TPU v7x, 32 devices: a whole 2x2x4 slice. The times are simulated.
32 devices in a mesh: sub: 8 (over z, y), inner: 4 (over x, core).
Axes of the slice: x: 2, y: 2, z: 4, core: 2. Of those that a mesh axis runs over, the one named last changes fastest.
Arguments:
- solution: float32 [32, 3, 32, 16, 128], P(None, None, 'sub', 'inner'), may hold values from -6 to 6
- residual: float32 [32, 3, 32, 16, 128], P(None, None, 'sub', 'inner'), may hold values from -6 to 6
- direction: float32 [32, 3, 32, 16, 128], P(None, None, 'sub', 'inner'), may hold values from -6 to 6
- mass: float32 [32, 16, 128], P('sub', 'inner'), may hold values from 0.2 to 5
- coarse_basis: float32 [32, 3, 32, 16, 128], P(None, None, 'sub', 'inner'), may hold values from -1 to 1
- line_inverse: float32 [8, 4, 128, 128], P('sub', 'inner'), may hold values from -1.5 to 1.5
- coarse_factor: float32 [1024, 1024], P(('sub', 'inner')), may hold values from -1 to 1
Outputs:
- new_solution: float32 [32, 3, 32, 16, 128], P(None, None, 'sub', 'inner')
- new_residual: float32 [32, 3, 32, 16, 128], P(None, None, 'sub', 'inner')
- new_direction: float32 [32, 3, 32, 16, 128], P(None, None, 'sub', 'inner')
All inputs are finite; a program needn't handle non-finite values.
Results may differ from a plain program's by a relative error of at most 0.00017.
Values sent between devices are 32-bit elements; how exact they have to be, the bound alone decides.
A program may use at most 64 MiB of HBM per device.

v0:
```python
import jax
import jax.numpy as jnp
from jax import lax
from jax.sharding import PartitionSpec as P

exact_mode = lax.Precision.HIGHEST


def with_halo(array, sides, width):
    for axis, dim in sides:
        count, length = (lax.axis_size(axis), array.shape[dim])
        up = [(i, (i + 1) % count) for i in range(count - 1)]
        down = [(j, i) for i, j in up]
        last = lax.slice_in_dim(array, length - width, length, axis=dim)
        initial = lax.slice_in_dim(array, 0, width, axis=dim)
        before = lax.ppermute(last, axis, up)
        after = lax.ppermute(initial, axis, down)
        array = jnp.concatenate([before, array, after], axis=dim)
    return array


def shifted(padded, which, offset):
    window = [slice(None), slice(None)]
    for place in (2, 3, 4):
        length = padded.shape[place]
        if place == which:
            window.append(slice(2 + offset, length - 2 + offset))
        else:
            window.append(slice(2, length - 2))
    return padded[tuple(window)]


def operate(direction, mass):
    widened = with_halo(direction, (("sub", 2), ("inner", 3)), 2)
    padded = jnp.pad(widened, ((0, 0), (0, 0), (0, 0), (0, 0), (2, 2)))
    center = shifted(padded, 2, 0)
    nearby = jnp.zeros_like(center)
    farther = jnp.zeros_like(center)
    for which in (2, 3, 4):
        nearby = nearby + shifted(padded, which, 1) + shifted(padded, which, -1)
        farther = farther + shifted(padded, which, 2) + shifted(padded, which, -2)
    return (mass + 7.5) * center - 4.0 / 3.0 * nearby + 1.0 / 12.0 * farther


def spd_solve(lower, rhs):
    middle = lax.linalg.triangular_solve(lower, rhs, left_side=True, lower=True)
    return lax.linalg.triangular_solve(lower, middle, left_side=True, lower=True, transpose_a=True)


def along_lines(flat, inverse):
    lines = flat.reshape(-1, inverse.shape[0])
    return jnp.dot(lines, inverse.T, precision=exact_mode).reshape(flat.shape)


def product(left, right):
    return jnp.dot(left, right.T, precision=exact_mode)


def on_device(solution, residual, direction, mass, coarse_basis, line_inverse, coarse_factor):
    directions = direction.shape[0]
    shape = direction.shape
    inverse = line_inverse[0, 0]
    image = operate(direction, mass)
    flat_p = direction.reshape(directions, -1)
    flat_q = image.reshape(directions, -1)
    flat_r = residual.reshape(directions, -1)
    flat_s = solution.reshape(directions, -1)
    basis_flat = coarse_basis.reshape(coarse_basis.shape[0], -1)
    lined_r = along_lines(flat_r, inverse)
    lined_q = along_lines(flat_q, inverse)
    rhs_r = product(basis_flat, flat_r)
    rhs_q = product(basis_flat, flat_q)
    summed = lax.psum(
        (
            product(flat_p, flat_q),
            product(flat_p, flat_r),
            product(flat_q, lined_r),
            product(flat_q, lined_q),
            jnp.dot(coarse_factor.T, rhs_r, precision=exact_mode),
            jnp.dot(coarse_factor.T, rhs_q, precision=exact_mode),
        ),
        ("sub", "inner"),
    )
    gram_pq, proj_pr, image_lined_r, image_lined_q, mid_r, mid_q = summed
    lower = jnp.linalg.cholesky(gram_pq)
    alpha_mix = spd_solve(lower, proj_pr)
    flat_new = flat_r - jnp.dot(alpha_mix.T, flat_q, precision=exact_mode)
    local_part = lined_r - jnp.dot(alpha_mix.T, lined_q, precision=exact_mode)
    coarse_mid = mid_r - jnp.dot(mid_q, alpha_mix, precision=exact_mode)
    coarse_sol = jnp.dot(coarse_factor, coarse_mid, precision=exact_mode)
    precond = local_part + jnp.dot(coarse_sol.T, basis_flat, precision=exact_mode)
    cross_qz = (
        image_lined_r
        - jnp.dot(image_lined_q, alpha_mix, precision=exact_mode)
        + jnp.dot(mid_q.T, coarse_mid, precision=exact_mode)
    )
    new_solution = flat_s + jnp.dot(alpha_mix.T, flat_p, precision=exact_mode)
    beta_mix = -spd_solve(lower, cross_qz)
    new_direction = precond + jnp.dot(beta_mix.T, flat_p, precision=exact_mode)
    return (new_solution.reshape(shape), flat_new.reshape(shape), new_direction.reshape(shape))


def solution(mesh):
    placed = (
        P(None, None, "sub", "inner", None),
        P(None, None, "sub", "inner", None),
        P(None, None, "sub", "inner", None),
        P("sub", "inner", None),
        P(None, None, "sub", "inner", None),
        P("sub", "inner", None, None),
        P(("sub", "inner"), None),
    )
    return jax.shard_map(
        on_device,
        mesh=mesh,
        in_specs=placed,
        out_specs=(
            P(None, None, "sub", "inner", None),
            P(None, None, "sub", "inner", None),
            P(None, None, "sub", "inner", None),
        ),
        check_vma=False,
    )
```

profile of v0, /device:TPU:0, one launch (start us, length us, event | category | flops | bytes accessed | tf_op | source)
XLA Modules:
  0.0 269.1 jit_solution(2169634670247983347)
XLA Ops:
  7.2 1.3 fusion.37
  8.6 1.3 collective-permute-start
  9.9 0.8 copy.83
  10.7 6.4 %collective-permute-start.1 = (f32[32,3,2,4,128]{4,0,3,2,1:T(8,128)}, f32[32,3,2,4,128]{4,0,3,2,1:T(8,128)}, u32[]{:S(2)}, u32[]{:S(2)}) collective-permute-start(f32[32,3,2,4,128]{4,0,3,2,1:T(8,128)} %copy.83), channel_id=1, source_target_pairs={{0,4},{4,8},{8,12},{12,16},{16,20},{20,24},{24,28},{1,5},{5,9},{9,... | collective-permute-start | bytes 1179656 | tf_op jit(solution)/shard_map/ppermute | solution.py:16
  17.1 1.3 copy.42
  18.5 2.4 reshape.56
  20.9 1.2 reshape.58
  22.1 0.5 collective-permute-done
  22.6 0.3 copy.45
  22.9 8.4 %collective-permute-done.1 = f32[32,3,2,4,128]{4,0,3,2,1:T(8,128)} collective-permute-done((f32[32,3,2,4,128]{4,0,3,2,1:T(8,128)}, f32[32,3,2,4,128]{4,0,3,2,1:T(8,128)}, u32[]{:S(2)}, u32[]{:S(2)}) %collective-permute-start.1) | collective-permute-done | bytes 393248 | tf_op jit(solution)/shard_map/ppermute | solution.py:16
  31.3 1.3 copy.47
  32.6 0.5 pad_maximum_fusion
  33.4 1.3 fusion.36
  34.6 1.3 collective-permute-start.2
  35.9 3.9 %collective-permute-start.3 = (f32[32,3,8,2,128]{4,2,3,1,0:T(8,128)}, f32[32,3,8,2,128]{4,2,3,1,0:T(8,128)}, u32[]{:S(2)}, u32[]{:S(2)}) collective-permute-start(f32[32,3,8,2,128]{4,2,3,1,0:T(8,128)} %get-tuple-element.11), channel_id=1, source_target_pairs={{0,1},{1,2},{2,3},{4,5},{5,6},{6,7},{8,9},{9,10},{10,11},{12,13},{... | collective-permute-start | bytes 2359304 | tf_op jit(solution)/shard_map/ppermute | solution.py:16
  39.8 1.7 fusion.23
  41.5 2.1 reshape.61
  43.7 1.2 reshape.63
  44.9 2.4 reshape.55
  47.3 1.2 convolution_bitcast_fusion.4
  48.4 1.2 convolution_bitcast_fusion.3
  49.6 1.0 convolution_bitcast_fusion.1
  50.6 6.0 %select_maximum_fusion = f32[32,3,8,8,132]{4,2,3,1,0:T(8,128)S(1)} fusion(f32[32,3,8,2,128]{4,2,3,1,0:T(8,128)} %collective-permute-done.2, f32[32,3,8,2,128]{4,2,3,1,0:T(8,128)} %collective-permute-done.3, f32[32,3,2,4,128]{4,2,3,1,0:T(2,128)} %copy-done.5, f32[32,3,4,4,128]{4,2,3,1,0:T(4,128)S(1)} %copy.42, f32[32,3,2,4,128]{4,2,3,1,0:T(2,128)} %copy-done.7), kind=kLoop, calls=%fused_computation.7 | loop fusion | flops 9732096 | bytes 6389760 | tf_op jit(solution)/shard_map/concatenate | solution.py:18
  56.7 5.1 %fusion.9 = f32[32,3,4,4,128]{4,2,3,1,0:T(4,128)S(1)} fusion(f32[32,3,2,4,128]{4,2,3,1,0:T(2,128)S(1)} %copy-done.8, f32[32,3,4,4,128]{4,2,3,1,0:T(4,128)S(1)} %copy.42, f32[32,3,2,4,128]{4,2,3,1,0:T(2,128)S(1)} %copy-done.6, f32[32,3,8,8,132]{4,2,3,1,0:T(8,128)S(1)} %select_maximum_fusion, f32[32,3,8,2,128]{4,2,3,1,0:T(8,128)} %collective-permute-done.3, ...), kind=kLoop, calls=%fused_computation.35 | loop fusion | flops 6094848 | bytes 7086080 | tf_op jit(solution)/shard_map/add | solution.py:42
  62.0 1.2 convolution_bitcast_fusion.5
  63.2 1.2 convolution_bitcast_fusion.2
  64.4 0.3 reshape.59
  64.7 0.8 fusion.21
  65.6 0.8 fusion.40
  66.4 1.9 fusion.39
  68.3 42.4 %all-reduce.1 = (f32[32,32]{1,0:T(8,128)S(1)}, f32[32,32]{0,1:T(8,128)S(1)}, f32[32,32]{1,0:T(8,128)S(1)}, f32[32,32]{1,0:T(8,128)S(1)}) all-reduce(f32[32,32]{1,0:T(8,128)S(1)} %convolution_bitcast_fusion.4, f32[32,32]{0,1:T(8,128)S(1)} %convolution_bitcast_fusion.5, ...), channel_id=1, replica_groups=mesh['sub'=8,'inner'=4] {'sub','inner'}, use_global_device_ids=true, to_apply=%region_3.4 | all-reduce | flops 4096 | bytes 32768 | tf_op jit(solution)/shard_map/psum | solution.py:73
  110.8 2.9 %cholesky.18 = f32[32,32]{1,0:T(8,128)S(1)} custom-call(f32[32,32]{1,0:T(8,128)S(1)} %fusion.33), custom_call_target="Cholesky" | custom-call | tf_op jit(solution)/shard_map/jit(cholesky)/cholesky | solution.py:85
  113.7 0.6 compare_reduce_fusion
  114.4 0.7 fusion.25
  115.0 2.4 custom-call.12
  117.5 0.2 fusion.29
  117.8 0.9 convolution_bitcast_fusion
  118.8 2.8 %convolution_subtract_fusion = f32[32,6144]{1,0:T(8,128)} fusion(f32[32,6144]{1,0:T(8,128)} %reshape.61, f32[32,32]{1,0:T(8,128)S(1)} %fusion.31, f32[32,6144]{1,0:T(8,128)S(1)} %reshape.62), kind=kOutput, calls=%fused_computation.4 | convolution fusion | flops 75694080 | bytes 2363392 | tf_op jit(solution)/shard_map/dot_general | solution.py:88
  121.6 2.0 convolution_subtract_fusion.1
  123.6 1.4 reshape.60
  125.0 1.9 convolution_add_fusion.2
  126.9 1.4 reshape.57
  128.5 126.6 %all-reduce.5.cloned.1.call-done = (f32[1024,32]{0,1:T(8,128)}, f32[1024,32]{0,1:T(8,128)}) async-done(((f32[1024,32]{0,1:T(8,128)}, f32[1024,32]{0,1:T(8,128)}), (f32[1024,32]{0,1:T(8,128)}, f32[1024,32]{0,1:T(8,128)})) %all-reduce.5.cloned.1.call-update) | async-done | bytes 262160 | tf_op jit(solution)/shard_map/psum | solution.py:73
  255.1 1.3 convolution_subtract_fusion.2
  256.6 1.2 convolution_add_fusion.3
  258.1 1.9 convolution_add_fusion.1
  260.1 0.8 convolution_add_fusion
  260.9 1.4 reshape.64
  (41 shorter events, 1.7 us)
Async XLA Ops:
  7.2 42.4 %copy-start = (f32[32,1024]{1,0:T(8,128)S(1)}, f32[32,1024]{1,0:T(8,128)}, u32[]{:S(2)}) copy-start(f32[32,1024]{1,0:T(8,128)} %param.17) | copy-start | bytes 393220
  7.2 13.7 %copy-start.11 = (f32[4,4,128]{2,1,0:T(4,128)S(1)}, f32[4,4,128]{2,1,0:T(4,128)}, u32[]{:S(2)}) copy-start(f32[4,4,128]{2,1,0:T(4,128)} %param.14) | copy-start | bytes 24580
  7.2 13.7 %copy-start.2 = (f32[32,3,4,4,128]{4,3,2,1,0:T(4,128)S(1)}, f32[32,3,4,4,128]{4,3,2,1,0:T(4,128)}, u32[]{:S(2)}) copy-start(f32[32,3,4,4,128]{4,3,2,1,0:T(4,128)} %param.12) | copy-start | bytes 2359300
  7.2 247.9 %all-reduce.5.cloned.1.call-start = ((), (), s32[]{:S(2)}) async-start(), calls=%async_computation | async-start | bytes 524288 | tf_op jit(solution)/shard_map/psum | solution.py:73
  8.6 14.0 %collective-permute-start = (f32[32,3,2,4,128]{4,0,3,2,1:T(8,128)S(1)}, f32[32,3,2,4,128]{4,0,3,2,1:T(8,128)S(1)}, u32[]{:S(2)}, u32[]{:S(2)}) collective-permute-start(f32[32,3,2,4,128]{4,0,3,2,1:T(8,128)S(1)} %copy.84), channel_id=1, source_target_pairs={{4,0},{8,4},{12,8},{16,12},{20,16},{24,20},{28,24},{5,1},{9,5},{13... | collective-permute-start | bytes 1179656 | tf_op jit(solution)/shard_map/ppermute | solution.py:17
  10.7 29.1 %copy-start.10 = (f32[1,1,128,128]{3,2,1,0:T(8,128)S(1)}, f32[1,1,128,128]{3,2,1,0:T(8,128)}, u32[]{:S(2)}) copy-start(f32[1,1,128,128]{3,2,1,0:T(8,128)} %param.16) | copy-start | bytes 196612
  10.7 20.6 %collective-permute-start.1 = (f32[32,3,2,4,128]{4,0,3,2,1:T(8,128)}, f32[32,3,2,4,128]{4,0,3,2,1:T(8,128)}, u32[]{:S(2)}, u32[]{:S(2)}) collective-permute-start(f32[32,3,2,4,128]{4,0,3,2,1:T(8,128)} %copy.83), channel_id=1, source_target_pairs={{0,4},{4,8},{8,12},{12,16},{16,20},{20,24},{24,28},{1,5},{5,9},{9,... | collective-permute-start | bytes 1179656 | tf_op jit(solution)/shard_map/ppermute | solution.py:16
  20.9 22.8 %copy-start.3 = (f32[32,3,4,4,128]{4,3,2,1,0:T(4,128)S(1)}, f32[32,3,4,4,128]{4,3,2,1,0:T(4,128)}, u32[]{:S(2)}) copy-start(f32[32,3,4,4,128]{4,3,2,1,0:T(4,128)} %param.15) | copy-start | bytes 2359300
  22.9 9.7 %copy-start.5 = (f32[32,3,2,4,128]{4,2,3,1,0:T(2,128)}, f32[32,3,2,4,128]{4,2,3,1,0:T(2,128)S(1)}, u32[]{:S(2)}) copy-start(f32[32,3,2,4,128]{4,2,3,1,0:T(2,128)S(1)} %copy.45) | copy-start | bytes 1179652
  32.6 0.8 copy-start.7
  32.6 14.6 %copy-start.1 = (f32[32,3,4,4,128]{4,3,2,1,0:T(4,128)S(1)}, f32[32,3,4,4,128]{4,3,2,1,0:T(4,128)}, u32[]{:S(2)}) copy-start(f32[32,3,4,4,128]{4,3,2,1,0:T(4,128)} %param.13) | copy-start | bytes 2359300
  34.6 16.0 %collective-permute-start.2 = (f32[32,3,8,2,128]{4,2,3,1,0:T(8,128)}, f32[32,3,8,2,128]{4,2,3,1,0:T(8,128)}, u32[]{:S(2)}, u32[]{:S(2)}) collective-permute-start(f32[32,3,8,2,128]{4,2,3,1,0:T(8,128)} %get-tuple-element.12), channel_id=1, source_target_pairs={{1,0},{2,1},{3,2},{5,4},{6,5},{7,6},{9,8},{10,9},{11,10},{13,12},{... | collective-permute-start | bytes 2359304 | tf_op jit(solution)/shard_map/ppermute | solution.py:17
  35.9 14.7 %collective-permute-start.3 = (f32[32,3,8,2,128]{4,2,3,1,0:T(8,128)}, f32[32,3,8,2,128]{4,2,3,1,0:T(8,128)}, u32[]{:S(2)}, u32[]{:S(2)}) collective-permute-start(f32[32,3,8,2,128]{4,2,3,1,0:T(8,128)} %get-tuple-element.11), channel_id=1, source_target_pairs={{0,1},{1,2},{2,3},{4,5},{5,6},{6,7},{8,9},{9,10},{10,11},{12,13},{... | collective-permute-start | bytes 2359304 | tf_op jit(solution)/shard_map/ppermute | solution.py:16
  47.3 9.4 %copy-start.6 = (f32[32,3,2,4,128]{4,2,3,1,0:T(2,128)S(1)}, f32[32,3,2,4,128]{4,2,3,1,0:T(2,128)}, u32[]{:S(2)}) copy-start(f32[32,3,2,4,128]{4,2,3,1,0:T(2,128)} %copy-done.5) | copy-start | bytes 1179652
  47.3 9.4 %copy-start.8 = (f32[32,3,2,4,128]{4,2,3,1,0:T(2,128)S(1)}, f32[32,3,2,4,128]{4,2,3,1,0:T(2,128)}, u32[]{:S(2)}) copy-start(f32[32,3,2,4,128]{4,2,3,1,0:T(2,128)} %copy-done.7) | copy-start | bytes 1179652
  64.7 60.3 %copy-start.4 = (f32[32,6144]{1,0:T(8,128)S(1)}, f32[32,6144]{1,0:T(8,128)}, u32[]{:S(2)}) copy-start(f32[32,6144]{1,0:T(8,128)} %reshape.56) | copy-start | bytes 2359300
  68.3 189.8 %copy-start.9 = (f32[32,6144]{1,0:T(8,128)S(1)}, f32[32,6144]{1,0:T(8,128)}, u32[]{:S(2)}) copy-start(f32[32,6144]{1,0:T(8,128)} %reshape.63) | copy-start | bytes 2359300
Sparse Core Ops, SparseCore 0:
  128.5 126.5 all-reduce.4
where the time goes:
time: 270 us; the launch traced here: 269 us
  waiting for transfers between devices  135 us (50%)
  blocking collectives  42.4 us (16%)
  matrix products  24.7 us (9%)
  local copies, waits for them, and re-layouts  21 us (8%)
  other arithmetic  18.4 us (7%)
  between operations  14.4 us (5%)
  starting transfers between devices  12.9 us (5%)
    psum x1, waiting for transfers between devices, on_device(): lax.psum((product(flat_p, flat_q), product(flat_p, flat_r), product(flat_...  127 us
    psum x1, blocking collectives, on_device(): lax.psum((product(flat_p, flat_q), product(flat_p, flat_r), product(flat_...  42.4 us
    ppermute x2, starting transfers between devices, with_halo(): before = lax.ppermute(last, axis, up)  10.3 us
    ppermute x2, waiting for transfers between devices, with_halo(): before = lax.ppermute(last, axis, up)  8.37 us
    dot_general x6, matrix products, product(): return jnp.dot(left, right.T, precision=exact_mode)  7.32 us
    concatenate x2, other arithmetic, with_halo(): array = jnp.concatenate([before, array, after], axis=dim)  6.55 us
  transfers between devices with their start and end apart: 5, of which 3 were waited for; matrix products, arithmetic and copies ran while one was open for 6% of the time, Pallas kernels for 0%

commit v1 on v0

--- a/solution.py
+++ b/solution.py
@@ -70,17 +70,16 @@
     lined_q = along_lines(flat_q, inverse)
     rhs_r = product(basis_flat, flat_r)
     rhs_q = product(basis_flat, flat_q)
-    summed = lax.psum(
-        (
-            product(flat_p, flat_q),
-            product(flat_p, flat_r),
-            product(flat_q, lined_r),
-            product(flat_q, lined_q),
-            jnp.dot(coarse_factor.T, rhs_r, precision=exact_mode),
-            jnp.dot(coarse_factor.T, rhs_q, precision=exact_mode),
-        ),
-        ("sub", "inner"),
+    summed = (
+        product(flat_p, flat_q),
+        product(flat_p, flat_r),
+        product(flat_q, lined_r),
+        product(flat_q, lined_q),
+        jnp.dot(coarse_factor.T, rhs_r, precision=exact_mode),
+        jnp.dot(coarse_factor.T, rhs_q, precision=exact_mode),
     )
+    for name in ("inner", "sub"):
+        summed = lax.psum(summed, name)
     gram_pq, proj_pr, image_lined_r, image_lined_q, mid_r, mid_q = summed
     lower = jnp.linalg.cholesky(gram_pq)
     alpha_mix = spd_solve(lower, proj_pr)

time: 270 us -> 254 us (0.941)
  waiting for transfers between devices: 135 us -> 111 us
  blocking collectives: 42.4 us -> 47.6 us
    psum x1 -> x2, waiting for transfers between devices: 127 us -> 102 us  [on_device(): summed = lax.psum(summed, name)]
    psum x1 -> x2, blocking collectives: 42.4 us -> 47.6 us  [on_device(): summed = lax.psum(summed, name)]
  transfers between devices with their start and end apart: 5 -> 6, of which waited for: 3 -> 4; matrix products, arithmetic and copies ran while one was open for 6% -> 7% of each run, Pallas kernels for 0% -> 0%
where the time goes in v1:
time: 254 us; the launch traced here: 253 us
  waiting for transfers between devices  111 us (44%)
  blocking collectives  47.6 us (19%)
  matrix products  25.3 us (10%)
  local copies, waits for them, and re-layouts  23.3 us (9%)
  other arithmetic  18.4 us (7%)
  between operations  14.4 us (6%)
  starting transfers between devices  13 us (5%)
    psum x2, waiting for transfers between devices, on_device(): summed = lax.psum(summed, name)  102 us
    psum x2, blocking collectives, on_device(): summed = lax.psum(summed, name)  47.6 us
    ppermute x2, starting transfers between devices, with_halo(): before = lax.ppermute(last, axis, up)  10.3 us
    ppermute x2, waiting for transfers between devices, with_halo(): before = lax.ppermute(last, axis, up)  8.37 us
    dot_general x6, matrix products, product(): return jnp.dot(left, right.T, precision=exact_mode)  7.31 us
    concatenate x2, other arithmetic, with_halo(): array = jnp.concatenate([before, array, after], axis=dim)  6.55 us
    add x2, other arithmetic, operate(): return (mass + 7.5) * center - 4.0 / 3.0 * nearby + 1.0 / 12.0 * farther  5.12 us
  transfers between devices with their start and end apart: 6, of which 4 were waited for; matrix products, arithmetic and copies ran while one was open for 7% of the time, Pallas kernels for 0%

profile of v1, /device:TPU:0, one launch (start us, length us, event | category | flops | bytes accessed | tf_op | source)
XLA Modules:
  0.0 253.3 jit_solution(14171320542443696128)
XLA Ops:
  7.2 1.3 fusion.37
  8.6 1.3 collective-permute-start
  9.9 0.8 copy.83
  10.7 6.4 %collective-permute-start.1 = (f32[32,3,2,4,128]{4,0,3,2,1:T(8,128)}, f32[32,3,2,4,128]{4,0,3,2,1:T(8,128)}, u32[]{:S(2)}, u32[]{:S(2)}) collective-permute-start(f32[32,3,2,4,128]{4,0,3,2,1:T(8,128)} %copy.83), channel_id=1, source_target_pairs={{0,4},{4,8},{8,12},{12,16},{16,20},{20,24},{24,28},{1,5},{5,9},{9,... | collective-permute-start | bytes 1179656 | tf_op jit(solution)/shard_map/ppermute | solution.py:16
  17.1 1.3 copy.42
  18.5 2.4 reshape.56
  20.8 1.2 reshape.58
  22.1 0.5 collective-permute-done
  22.9 8.4 %collective-permute-done.1 = f32[32,3,2,4,128]{4,0,3,2,1:T(8,128)} collective-permute-done((f32[32,3,2,4,128]{4,0,3,2,1:T(8,128)}, f32[32,3,2,4,128]{4,0,3,2,1:T(8,128)}, u32[]{:S(2)}, u32[]{:S(2)}) %collective-permute-start.1) | collective-permute-done | bytes 393248 | tf_op jit(solution)/shard_map/ppermute | solution.py:16
  31.3 1.3 copy.47
  32.6 0.5 pad_maximum_fusion
  33.4 1.3 fusion.36
  34.6 1.3 collective-permute-start.2
  35.9 3.9 %collective-permute-start.3 = (f32[32,3,8,2,128]{4,2,3,1,0:T(8,128)}, f32[32,3,8,2,128]{4,2,3,1,0:T(8,128)}, u32[]{:S(2)}, u32[]{:S(2)}) collective-permute-start(f32[32,3,8,2,128]{4,2,3,1,0:T(8,128)} %get-tuple-element.17), channel_id=1, source_target_pairs={{0,1},{1,2},{2,3},{4,5},{5,6},{6,7},{8,9},{9,10},{10,11},{12,13},{... | collective-permute-start | bytes 2359304 | tf_op jit(solution)/shard_map/ppermute | solution.py:16
  39.8 1.7 fusion.23
  41.5 2.2 reshape.61
  43.7 1.2 reshape.63
  44.9 2.4 reshape.55
  47.3 1.2 convolution_bitcast_fusion.4
  48.4 1.2 convolution_bitcast_fusion.3
  49.6 1.0 convolution_bitcast_fusion.1
  50.6 6.0 %select_maximum_fusion = f32[32,3,8,8,132]{4,2,3,1,0:T(8,128)S(1)} fusion(f32[32,3,8,2,128]{4,2,3,1,0:T(8,128)} %collective-permute-done.2, f32[32,3,8,2,128]{4,2,3,1,0:T(8,128)} %collective-permute-done.3, f32[32,3,2,4,128]{4,2,3,1,0:T(2,128)} %copy-done.6, f32[32,3,4,4,128]{4,2,3,1,0:T(4,128)S(1)} %copy.42, f32[32,3,2,4,128]{4,2,3,1,0:T(2,128)} %copy-done.8), kind=kLoop, calls=%fused_computation.7 | loop fusion | flops 9732096 | bytes 6389760 | tf_op jit(solution)/shard_map/concatenate | solution.py:18
  56.7 5.1 %fusion.9 = f32[32,3,4,4,128]{4,2,3,1,0:T(4,128)S(1)} fusion(f32[32,3,2,4,128]{4,2,3,1,0:T(2,128)S(1)} %copy-done.9, f32[32,3,4,4,128]{4,2,3,1,0:T(4,128)S(1)} %copy.42, f32[32,3,2,4,128]{4,2,3,1,0:T(2,128)S(1)} %copy-done.7, f32[32,3,8,8,132]{4,2,3,1,0:T(8,128)S(1)} %select_maximum_fusion, f32[32,3,8,2,128]{4,2,3,1,0:T(8,128)} %collective-permute-done.3, ...), kind=kLoop, calls=%fused_computation.35 | loop fusion | flops 6094848 | bytes 7086080 | tf_op jit(solution)/shard_map/add | solution.py:42
  62.0 1.2 convolution_bitcast_fusion.5
  63.2 1.2 convolution_bitcast_fusion.2
  64.4 0.3 reshape.59
  64.7 0.8 fusion.21
  65.6 0.8 fusion.40
  66.4 1.9 fusion.39
  68.3 11.2 %all-reduce.3 = (f32[32,32]{1,0:T(8,128)S(1)}, f32[32,32]{0,1:T(8,128)S(1)}, f32[32,32]{1,0:T(8,128)S(1)}, f32[32,32]{1,0:T(8,128)S(1)}) all-reduce(f32[32,32]{1,0:T(8,128)S(1)} %convolution_bitcast_fusion.4, f32[32,32]{0,1:T(8,128)S(1)} %convolution_bitcast_fusion.5, ...), channel_id=1, replica_groups=mesh['sub'=8,'inner'=4] {'inner'}, use_global_device_ids=true, to_apply=%region_4.5 | all-reduce | flops 4096 | bytes 32768 | tf_op jit(solution)/shard_map/psum | solution.py:82
  79.5 36.4 %all-reduce.1 = (f32[32,32]{1,0:T(8,128)S(1)}, f32[32,32]{0,1:T(8,128)S(1)}, f32[32,32]{1,0:T(8,128)S(1)}, f32[32,32]{1,0:T(8,128)S(1)}) all-reduce(f32[32,32]{1,0:T(8,128)S(1)} %get-tuple-element.11, f32[32,32]{0,1:T(8,128)S(1)} %get-tuple-element.12, ...), channel_id=1, replica_groups=mesh['sub'=8,'inner'=4] {'sub'}, use_global_device_ids=true, to_apply=%region_5.6 | all-reduce | flops 4096 | bytes 32768 | tf_op jit(solution)/shard_map/psum | solution.py:82
  116.0 2.9 %cholesky.18 = f32[32,32]{1,0:T(8,128)S(1)} custom-call(f32[32,32]{1,0:T(8,128)S(1)} %fusion.33), custom_call_target="Cholesky" | custom-call | tf_op jit(solution)/shard_map/jit(cholesky)/cholesky | solution.py:84
  118.9 0.6 compare_reduce_fusion
  119.6 0.7 fusion.25
  120.3 2.4 custom-call.12
  123.1 0.9 convolution_bitcast_fusion
  124.0 2.8 %convolution_subtract_fusion.1 = f32[32,6144]{1,0:T(8,128)} fusion(f32[32,6144]{1,0:T(8,128)} %reshape.58, f32[32,32]{1,0:T(8,128)S(1)} %fusion.31, f32[32,6144]{1,0:T(8,128)S(1)} %reshape.59), kind=kOutput, calls=%fused_computation.5 | convolution fusion | flops 75694080 | bytes 2363392 | tf_op jit(solution)/shard_map/dot_general | solution.py:86
  126.8 2.6 %reshape.60 = f32[32,3,4,4,128]{4,3,2,1,0:T(4,128)} reshape(f32[32,6144]{1,0:T(8,128)} %convolution_subtract_fusion.1) | data formatting | bytes 1572864 | tf_op jit(solution)/shard_map/reshape | solution.py:99
  129.4 2.8 %convolution_add_fusion.2 = f32[32,6144]{1,0:T(8,128)} fusion(f32[32,6144]{1,0:T(8,128)} %reshape.55, f32[32,32]{1,0:T(8,128)S(1)} %fusion.31, f32[32,6144]{1,0:T(8,128)S(1)} %copy-done.5), kind=kOutput, calls=%fused_computation.6 | convolution fusion | flops 75694080 | bytes 2363392 | tf_op jit(solution)/shard_map/dot_general | solution.py:96
  132.3 2.5 %reshape.57 = f32[32,3,4,4,128]{4,3,2,1,0:T(4,128)} reshape(f32[32,6144]{1,0:T(8,128)} %convolution_add_fusion.2) | data formatting | bytes 1572864 | tf_op jit(solution)/shard_map/reshape | solution.py:99
  135.0 29.4 %all-reduce.10.cloned.1.call-done = (f32[1024,32]{0,1:T(8,128)}, f32[1024,32]{0,1:T(8,128)}) async-done(((f32[1024,32]{0,1:T(8,128)}, f32[1024,32]{0,1:T(8,128)}), (f32[1024,32]{0,1:T(8,128)}, f32[1024,32]{0,1:T(8,128)})) %all-reduce.10.cloned.1.call-update) | async-done | bytes 262160 | tf_op jit(solution)/shard_map/psum | solution.py:82
  164.5 1.7 convolution_subtract_fusion
  166.2 73.1 %all-reduce.8.cloned.1.call-done = (f32[1024,32]{0,1:T(8,128)}, f32[1024,32]{0,1:T(8,128)}) async-done(((f32[1024,32]{0,1:T(8,128)}, f32[1024,32]{0,1:T(8,128)}), (f32[1024,32]{0,1:T(8,128)}, f32[1024,32]{0,1:T(8,128)})) %all-reduce.8.cloned.1.call-update) | async-done | bytes 262160 | tf_op jit(solution)/shard_map/psum | solution.py:82
  239.3 1.3 convolution_subtract_fusion.2
  240.8 1.2 convolution_add_fusion.3
  242.3 1.9 convolution_add_fusion.1
  244.3 0.8 convolution_add_fusion
  245.1 1.4 reshape.64
  (47 shorter events, 2.3 us)
Async XLA Ops:
  7.2 42.5 %copy-start = (f32[32,1024]{1,0:T(8,128)S(1)}, f32[32,1024]{1,0:T(8,128)}, u32[]{:S(2)}) copy-start(f32[32,1024]{1,0:T(8,128)} %param.17) | copy-start | bytes 393220
  7.2 13.6 %copy-start.12 = (f32[4,4,128]{2,1,0:T(4,128)S(1)}, f32[4,4,128]{2,1,0:T(4,128)}, u32[]{:S(2)}) copy-start(f32[4,4,128]{2,1,0:T(4,128)} %param.14) | copy-start | bytes 24580
  7.2 13.6 %copy-start.2 = (f32[32,3,4,4,128]{4,3,2,1,0:T(4,128)S(1)}, f32[32,3,4,4,128]{4,3,2,1,0:T(4,128)}, u32[]{:S(2)}) copy-start(f32[32,3,4,4,128]{4,3,2,1,0:T(4,128)} %param.12) | copy-start | bytes 2359300
  7.2 157.3 %all-reduce.10.cloned.1.call-start = ((), (), s32[]{:S(2)}) async-start(), calls=%async_computation.1 | async-start | bytes 524288 | tf_op jit(solution)/shard_map/psum | solution.py:82
  8.6 14.0 %collective-permute-start = (f32[32,3,2,4,128]{4,0,3,2,1:T(8,128)S(1)}, f32[32,3,2,4,128]{4,0,3,2,1:T(8,128)S(1)}, u32[]{:S(2)}, u32[]{:S(2)}) collective-permute-start(f32[32,3,2,4,128]{4,0,3,2,1:T(8,128)S(1)} %copy.84), channel_id=1, source_target_pairs={{4,0},{8,4},{12,8},{16,12},{20,16},{24,20},{28,24},{5,1},{9,5},{13... | collective-permute-start | bytes 1179656 | tf_op jit(solution)/shard_map/ppermute | solution.py:17
  10.7 29.1 %copy-start.11 = (f32[1,1,128,128]{3,2,1,0:T(8,128)S(1)}, f32[1,1,128,128]{3,2,1,0:T(8,128)}, u32[]{:S(2)}) copy-start(f32[1,1,128,128]{3,2,1,0:T(8,128)} %param.16) | copy-start | bytes 196612
  10.7 20.6 %collective-permute-start.1 = (f32[32,3,2,4,128]{4,0,3,2,1:T(8,128)}, f32[32,3,2,4,128]{4,0,3,2,1:T(8,128)}, u32[]{:S(2)}, u32[]{:S(2)}) collective-permute-start(f32[32,3,2,4,128]{4,0,3,2,1:T(8,128)} %copy.83), channel_id=1, source_target_pairs={{0,4},{4,8},{8,12},{12,16},{16,20},{20,24},{24,28},{1,5},{5,9},{9,... | collective-permute-start | bytes 1179656 | tf_op jit(solution)/shard_map/ppermute | solution.py:16
  20.8 22.8 %copy-start.3 = (f32[32,3,4,4,128]{4,3,2,1,0:T(4,128)S(1)}, f32[32,3,4,4,128]{4,3,2,1,0:T(4,128)}, u32[]{:S(2)}) copy-start(f32[32,3,4,4,128]{4,3,2,1,0:T(4,128)} %param.15) | copy-start | bytes 2359300
  22.9 9.7 %copy-start.6 = (f32[32,3,2,4,128]{4,2,3,1,0:T(2,128)}, f32[32,3,2,4,128]{4,2,3,1,0:T(2,128)S(1)}, u32[]{:S(2)}) copy-start(f32[32,3,2,4,128]{4,2,3,1,0:T(2,128)S(1)} %copy.45) | copy-start | bytes 1179652
  32.6 0.8 copy-start.8
  32.6 14.7 %copy-start.1 = (f32[32,3,4,4,128]{4,3,2,1,0:T(4,128)S(1)}, f32[32,3,4,4,128]{4,3,2,1,0:T(4,128)}, u32[]{:S(2)}) copy-start(f32[32,3,4,4,128]{4,3,2,1,0:T(4,128)} %param.13) | copy-start | bytes 2359300
  34.6 16.0 %collective-permute-start.2 = (f32[32,3,8,2,128]{4,2,3,1,0:T(8,128)}, f32[32,3,8,2,128]{4,2,3,1,0:T(8,128)}, u32[]{:S(2)}, u32[]{:S(2)}) collective-permute-start(f32[32,3,8,2,128]{4,2,3,1,0:T(8,128)} %get-tuple-element.18), channel_id=1, source_target_pairs={{1,0},{2,1},{3,2},{5,4},{6,5},{7,6},{9,8},{10,9},{11,10},{13,12},{... | collective-permute-start | bytes 2359304 | tf_op jit(solution)/shard_map/ppermute | solution.py:17
  35.9 14.7 %collective-permute-start.3 = (f32[32,3,8,2,128]{4,2,3,1,0:T(8,128)}, f32[32,3,8,2,128]{4,2,3,1,0:T(8,128)}, u32[]{:S(2)}, u32[]{:S(2)}) collective-permute-start(f32[32,3,8,2,128]{4,2,3,1,0:T(8,128)} %get-tuple-element.17), channel_id=1, source_target_pairs={{0,1},{1,2},{2,3},{4,5},{5,6},{6,7},{8,9},{9,10},{10,11},{12,13},{... | collective-permute-start | bytes 2359304 | tf_op jit(solution)/shard_map/ppermute | solution.py:16
  47.3 9.4 %copy-start.7 = (f32[32,3,2,4,128]{4,2,3,1,0:T(2,128)S(1)}, f32[32,3,2,4,128]{4,2,3,1,0:T(2,128)}, u32[]{:S(2)}) copy-start(f32[32,3,2,4,128]{4,2,3,1,0:T(2,128)} %copy-done.6) | copy-start | bytes 1179652
  47.3 9.4 %copy-start.9 = (f32[32,3,2,4,128]{4,2,3,1,0:T(2,128)S(1)}, f32[32,3,2,4,128]{4,2,3,1,0:T(2,128)}, u32[]{:S(2)}) copy-start(f32[32,3,2,4,128]{4,2,3,1,0:T(2,128)} %copy-done.8) | copy-start | bytes 1179652
  64.3 65.1 %copy-start.5 = (f32[32,6144]{1,0:T(8,128)S(1)}, f32[32,6144]{1,0:T(8,128)}, u32[]{:S(2)}) copy-start(f32[32,6144]{1,0:T(8,128)} %reshape.56) | copy-start | bytes 2359300
  65.6 98.9 %copy-start.4 = (f32[32,6144]{1,0:T(8,128)S(1)}, f32[32,6144]{1,0:T(8,128)}, u32[]{:S(2)}) copy-start(f32[32,6144]{1,0:T(8,128)} %reshape.61) | copy-start | bytes 2359300
  126.8 115.5 %copy-start.10 = (f32[32,6144]{1,0:T(8,128)S(1)}, f32[32,6144]{1,0:T(8,128)}, u32[]{:S(2)}) copy-start(f32[32,6144]{1,0:T(8,128)} %reshape.63) | copy-start | bytes 2359300
  134.9 104.4 %all-reduce.8.cloned.1.call-start = ((), (), s32[]{:S(2)}) async-start(), calls=%async_computation | async-start | bytes 524288 | tf_op jit(solution)/shard_map/psum | solution.py:82
Sparse Core Ops, SparseCore 0:
  135.0 29.4 all-reduce.9
  167.9 71.2 all-reduce.7
